TPU v7x, 128 devices: a whole 4x4x4 slice. The times are simulated.
128 devices in a mesh: row: 8 (over y, x_hi), col: 16 (over x_lo, z, core).
Axes of the slice: x: 4 (x_hi: 2, x_lo: 2; x = x_hi * 2 + x_lo), y: 4, z: 4, core: 2. Of those that a mesh axis runs over, the one named last changes fastest.
Arguments:
- left_matrix: float32 [4096, 4096], P('row', 'col'), may hold values from -6 to 6
- right_matrix: float32 [4096, 4096], P('row', 'col'), may hold values from -0.09375 to 0.09375
Outputs:
- product_matrix: float32 [4096, 4096], P('row', 'col')
All inputs are finite; a program needn't handle non-finite values.
Results may differ from a plain program's by a relative error of at most 0.00019.
Values sent between devices are 32-bit elements; how exact they have to be, the bound alone decides.
A program may use at most 64 MiB of HBM per device.

v0:
```python
import jax
import jax.numpy as jnp
from jax import lax
from jax.sharding import PartitionSpec as P


def copy_for_each(array, axis):
    devices = lax.axis_size(axis)
    return lax.all_to_all(
        jnp.broadcast_to(array[None], (devices, *array.shape)), axis, 0, 0, tiled=True
    )


def joined_along(pieces, dim):
    lengths = list(pieces.shape[1:])
    lengths[dim] *= pieces.shape[0]
    return jnp.moveaxis(pieces, 0, dim).reshape(lengths)


def collect(array, axis, dim):
    pieces = copy_for_each(array, axis)
    return joined_along(pieces, dim)


def multiply(left_term, right_term):
    return jnp.dot(
        left_term, right_term, precision=lax.Precision.HIGHEST, preferred_element_type=jnp.float32
    )


def body(left_matrix, right_matrix):
    row_panel = lax.all_gather(left_matrix, "col", axis=1, tiled=True)
    col_panel = collect(right_matrix, "row", 0)
    return multiply(row_panel, col_panel)


def solution(mesh):
    placed = (P("row", "col"), P("row", "col"))
    return jax.shard_map(
        body, mesh=mesh, in_specs=placed, out_specs=P("row", "col"), check_vma=False
    )
```

profile of v0, /device:TPU:1, one launch (start us, length us, event | category | flops | bytes accessed | tf_op | source)
XLA Modules:
  0.0 122.2 jit_solution(261679742766452399)
XLA Ops:
  6.5 0.0 all-gather.2.cloned.1.call-start
  6.5 0.7 all-gather.2.cloned.1.call-update
  7.3 1.4 %broadcast_in_dim.2 = f32[8,512,256]{2,1,0:T(8,128)S(1)} broadcast(f32[512,256]{1,0:T(8,128)} %param.3), dimensions={1,2} | broadcast | bytes 4718592 | tf_op jit(solution)/shard_map/broadcast_in_dim | solution.py:10
  8.7 96.2 %all_to_all.5 = f32[8,512,256]{2,1,0:T(8,128)} all-to-all(f32[8,512,256]{2,1,0:T(8,128)S(1)} %broadcast_in_dim.2), channel_id=1, replica_groups=mesh['row'=8,'col'=16] {'row'}, dimensions={0} | all-to-all | bytes 8388608 | tf_op jit(solution)/shard_map/all_to_all | solution.py:9
  104.8 0.0 all-gather.2.cloned.1.call-done
  104.8 10.6 %fusion = f32[512,256]{1,0:T(8,128)} fusion(f32[512,4096]{1,0:T(8,128)} %all-gather.2.cloned.1.call-done, f32[4096,256]{1,0:T(8,128)} %bitcast.3), kind=kOutput, calls=%fused_computation | convolution fusion | flops 6442450944 | bytes 13107200 | tf_op jit(solution)/shard_map/dot_general | solution.py:26
Async XLA Ops:
  6.5 98.3 %all-gather.2.cloned.1.call-start = ((), (), s32[]{:S(2)}) async-start(), calls=%async_computation.1 | async-start | bytes 8912896 | tf_op jit(solution)/shard_map/all_gather | solution.py:32
Sparse Core Ops, SparseCore 0:
  9.0 94.2 all-gather.1
where the time goes:
time: 123 us; the launch traced here: 122 us
  blocking collectives  96.2 us (78%)
  between operations  13.4 us (11%)
  matrix products  10.6 us (9%)
  local copies, waits for them, and re-layouts  1.4 us (1%)
    all_to_all x1, blocking collectives, copy_for_each(): lax.all_to_all(jnp.broadcast_to(array[None], (devices, *array.shape)), ax...  96.2 us
    dot_general x1, matrix products, multiply(): jnp.dot(left_term, right_term, precision=lax.Precision.HIGHEST, preferred...  10.6 us
  transfers between devices with their start and end apart: 1, of which 0 were waited for; matrix products, arithmetic and copies ran while one was open for 1% of the time, Pallas kernels for 0%

commit v1 on v0

v1 whole, which is shorter than its diff:
```python
import functools

import jax
import jax.numpy as jnp
from jax import lax
from jax.experimental import pallas as pl
from jax.experimental.pallas import tpu as pltpu
from jax.sharding import PartitionSpec as P

MESH = pl.DeviceIdType.MESH
CHUNKS = 4


def kernel(a_hbm, b_hbm, c_ref, a_buf, b_buf, relay, load_sem, a_sem, b_sem, relay_sem, send_sem):
    row, col = lax.axis_index("row"), lax.axis_index("col")
    y, x_hi = row // 2, row % 2
    x_lo, z, core = col // 8, (col // 2) % 4, col % 2
    x = x_hi * 2 + x_lo

    def device(x, y, z, core):
        return (y * 2 + x // 2, ((x % 2) * 4 + z) * 2 + core)

    z_up, z_down = device(x, y, (z + 1) % 4, core), device(x, y, (z + 3) % 4, core)
    y_up, y_down = device(x, (y + 1) % 4, z, core), device(x, (y + 3) % 4, z, core)
    x_pair = device(x_hi * 2 + 1 - x_lo, y, z, core)
    x_next = device(3 - x, y, z, core)
    twin = device(x, y, z, 1 - core)

    load_a = pltpu.make_async_copy(a_hbm, a_buf.at[0, 0], load_sem.at[0])
    load_b = pltpu.make_async_copy(b_hbm, b_buf.at[0], load_sem.at[1])
    load_a.start()
    load_b.start()

    barrier = pltpu.get_barrier_semaphore()
    for other in (z_up, z_down, y_up, y_down, x_pair, x_next, twin):
        pl.semaphore_signal(barrier, inc=1, device_id=other, device_id_type=MESH)
    c_ref[...] = jnp.zeros_like(c_ref)
    load_a.wait()
    load_b.wait()
    pl.semaphore_wait(barrier, 7)

    rows = a_buf.shape[2] // CHUNKS
    sent = []

    def send(src, dst, sem, to):
        copy = pltpu.make_async_remote_copy(
            src_ref=src,
            dst_ref=dst,
            send_sem=send_sem.at[len(sent)],
            recv_sem=sem,
            device_id=to,
            device_id_type=MESH,
        )
        copy.start()
        sent.append(copy)

    def part(q):
        return pl.ds(q * rows, rows)

    def a_send(src, q, slot, to):
        send(a_buf.at[0, src, part(q)], a_buf.at[0, slot, part(q)], a_sem.at[0, slot, q], to)

    def b_send(src, q, slot, to):
        send(b_buf.at[src, part(q)], b_buf.at[slot, part(q)], b_sem.at[slot, q], to)

    def a_twin(slot, q):
        send(a_buf.at[0, slot, part(q)], a_buf.at[1, slot, part(q)], a_sem.at[1, slot, q], twin)

    def a_wait(stream, slot, q):
        ref = a_buf.at[stream, slot, part(q)]
        pltpu.make_async_copy(ref, ref, a_sem.at[stream, slot, q]).wait()

    def b_wait(slot, q):
        ref = b_buf.at[slot, part(q)]
        pltpu.make_async_copy(ref, ref, b_sem.at[slot, q]).wait()

    def multiply(stage):
        @pl.loop(0, 8)
        def _(slot):
            d_x, d_z = slot // 4, slot % 4
            where = ((x_lo + d_x) % 2) * 4 + (z + d_z) % 4
            d_h, d_y = (where % 2 + x_hi) % 2, (where // 2 + 4 - y) % 4

            def stage_of(far, around):
                return jnp.where(far == 0, 1, jnp.where(around == 0, 2, jnp.where(around == 2, 4, 3)))

            ready = jnp.maximum(stage_of(d_x, d_z), stage_of(d_h, d_y))

            @pl.when(ready == stage)
            def _():
                for stream in range(2):
                    side = core if stream == 0 else 1 - core
                    b = b_buf[d_h * 4 + d_y, pl.ds(pl.multiple_of(side * 256, 256), 256)]
                    b_top = b.astype(jnp.bfloat16)
                    b_low = (b - b_top.astype(jnp.float32)).astype(jnp.bfloat16)
                    a = a_buf[stream, slot]
                    a_top = a.astype(jnp.bfloat16)
                    a_low = (a - a_top.astype(jnp.float32)).astype(jnp.bfloat16)
                    dot = functools.partial(jnp.dot, preferred_element_type=jnp.float32)
                    c_ref[...] += dot(a_top, b_top) + (dot(a_top, b_low) + dot(a_low, b_top))

    for q, p in zip((0, 1, 2, 3), (2, 3, 0, 1)):
        a_send(0, q, 3, z_up)
        a_send(0, p, 1, z_down)
        b_send(0, q, 3, y_up)
        b_send(0, p, 1, y_down)
        if q < 2:
            send(b_buf.at[0, part(q)], relay.at[0, q], relay_sem.at[0, q], x_pair)
            send(b_buf.at[0, part(q + 2)], relay.at[1, q], relay_sem.at[1, q], x_next)
    for q in range(3):
        a_send(0, q, 4, x_pair)
    for q in range(4):
        a_twin(0, q)

    for q in range(2):
        for which, to in ((0, x_next), (1, x_pair)):
            ref = relay.at[which, q]
            pltpu.make_async_copy(ref, ref, relay_sem.at[which, q]).wait()
            q_to = q + 2 * which
            send(ref, b_buf.at[4, part(q_to)], b_sem.at[4, q_to], to)
        a_wait(0, 3, q)
        a_send(3, q, 2, z_up)
        a_twin(3, q)
        a_wait(0, 1, q + 2)
        a_send(1, q + 2, 2, z_down)
        a_twin(1, q + 2)
        b_wait(3, q)
        b_send(3, q, 2, y_up)
        b_wait(1, q + 2)
        b_send(1, q + 2, 2, y_down)
    a_send(0, 3, 4, x_pair)

    for q in range(2):
        a_wait(0, 3, q + 2)
        a_twin(3, q + 2)
        a_wait(0, 1, q)
        a_twin(1, q)
        b_wait(3, q + 2)
        b_wait(1, q)
        a_wait(0, 4, q)
        a_send(4, q, 7, z_up)
        a_send(4, q, 5, z_down)
        a_twin(4, q)
        b_wait(4, q)
        b_send(4, q, 7, y_up)
        b_send(4, q, 5, y_down)
    for q in range(2, 4):
        a_wait(0, 4, q)
        a_send(4, q, 7, z_up)
        a_send(4, q, 5, z_down)
        a_twin(4, q)
        a_wait(0, 2, q - 2)
        a_twin(2, q - 2)
        a_wait(0, 2, q)
        a_twin(2, q)
        b_wait(2, q - 2)
        b_wait(2, q)
        b_wait(4, q)
        b_send(4, q, 7, y_up)
        b_send(4, q, 5, y_down)
    for slot in (0, 3, 1, 2):
        for q in range(4):
            a_wait(1, slot, q)
    multiply(1)
    for q in range(4):
        a_wait(1, 4, q)
    multiply(2)

    for q in range(4):
        a_wait(0, 7, q)
        if q < 2:
            a_send(7, q, 6, z_up)
        a_twin(7, q)
        a_wait(0, 5, q)
        if q >= 2:
            a_send(5, q, 6, z_down)
        a_twin(5, q)
        b_wait(7, q)
        if q < 2:
            b_send(7, q, 6, y_up)
        b_wait(5, q)
        if q >= 2:
            b_send(5, q, 6, y_down)
    for slot in (7, 5):
        for q in range(4):
            a_wait(1, slot, q)
    multiply(3)

    for q in (0, 2, 1, 3):
        a_wait(0, 6, q)
        a_twin(6, q)
        b_wait(6, q)
    for q in (0, 2, 1, 3):
        a_wait(1, 6, q)
    multiply(4)
    for copy in sent:
        copy.wait_send()


SENDS = 24 + 4 + 32 + 24 + 4 + 4


def body(left_matrix, right_matrix):
    rows, columns = left_matrix.shape
    part = rows // CHUNKS
    return pl.pallas_call(
        kernel,
        out_shape=jax.ShapeDtypeStruct((rows, columns), jnp.float32),
        in_specs=[pl.BlockSpec(memory_space=pl.ANY)] * 2,
        out_specs=pl.BlockSpec(memory_space=pltpu.VMEM),
        scratch_shapes=[
            pltpu.VMEM((2, 8, rows, columns), jnp.float32),
            pltpu.VMEM((8, rows, columns), jnp.float32),
            pltpu.VMEM((2, 2, part, columns), jnp.float32),
            pltpu.SemaphoreType.DMA((2,)),
            pltpu.SemaphoreType.DMA((2, 8, CHUNKS)),
            pltpu.SemaphoreType.DMA((8, CHUNKS)),
            pltpu.SemaphoreType.DMA((2, 2)),
            pltpu.SemaphoreType.DMA((SENDS,)),
        ],
        compiler_params=pltpu.CompilerParams(collective_id=0, has_side_effects=True),
    )(left_matrix, right_matrix)


def solution(mesh):
    placed = (P("row", "col"), P("row", "col"))
    return jax.shard_map(
        body, mesh=mesh, in_specs=placed, out_specs=P("row", "col"), check_vma=False
    )
```

time: 123 us -> 49 us (0.40)
  blocking collectives: 96.2 us -> 0 us
  Pallas kernels: 0 us -> 46.8 us
  between operations: 13.4 us -> 0.01 us
  matrix products: 10.6 us -> 0 us
    all_to_all x1 -> x0, blocking collectives: 96.2 us -> none  [copy_for_each(): lax.all_to_all(jnp.broadcast_to(array[None], (devices, *array.shape)), ax...]
    pallas_call x0 -> x1, Pallas kernels: none -> 46.8 us  [body(): pl.pallas_call(kernel, out_shape=jax.ShapeDtypeStruct((rows, columns), jn...]
    dot_general x1 -> x0, matrix products: 10.6 us -> none  [multiply(): jnp.dot(left_term, right_term, precision=lax.Precision.HIGHEST, preferred...]
    unnamed x0 -> x1, local copies, waits for them, and re-layouts: none -> 1.87 us
    broadcast_in_dim x1 -> x0, local copies, waits for them, and re-layouts: 1.4 us -> none  [copy_for_each(): jnp.broadcast_to(array[None], (devices, *array.shape))]
  transfers between devices with their start and end apart: 1 -> 0, of which waited for: 0 -> 0; matrix products, arithmetic and copies ran while one was open for 1% -> 0% of each run, Pallas kernels for 0% -> 0%
where the time goes in v1:
time: 49 us; the launch traced here: 48.7 us
  Pallas kernels  46.8 us (96%)
  local copies, waits for them, and re-layouts  1.87 us (4%)
    pallas_call x1, Pallas kernels, body(): pl.pallas_call(kernel, out_shape=jax.ShapeDtypeStruct((rows, columns), jn...  46.8 us
    unnamed x1, local copies, waits for them, and re-layouts  1.87 us

profile of v1, /device:TPU:1, one launch (start us, length us, event | category | flops | bytes accessed | tf_op | source)
XLA Modules:
  0.0 48.7 jit_solution(15243117293067498963)
XLA Ops:
  0.0 46.8 %shard_map.28 = f32[512,256]{1,0:T(8,128)} custom-call(f32[512,256]{1,0:T(8,128)} %a_hbm.1, f32[512,256]{1,0:T(8,128)} %b_hbm.1), custom_call_target="tpu_custom_call" | custom-call | tf_op jit(solution)/shard_map/pallas_call | solution.py:206
  46.8 1.9 %copy.4 = f32[512,256]{1,0:T(8,128)} copy(f32[512,256]{1,0:T(8,128)} %shard_map.28) | data formatting | bytes 1048576

commit v2 on v0

v2 whole, which is shorter than its diff:
```python
import functools

import jax
import jax.numpy as jnp
from jax import lax
from jax.experimental import pallas as pl
from jax.experimental.pallas import tpu as pltpu
from jax.sharding import PartitionSpec as P

MESH = pl.DeviceIdType.MESH
ROWS, COLUMNS = 512, 256
A_PARTS = {"U0": (0, 64), "U1": (64, 64), "D0": (128, 64), "D1": (192, 64), "X0": (256, 128), "X1": (384, 128)}
B_PARTS = {"U0": (0, 64), "U1": (64, 64), "D0": (128, 64), "D1": (192, 64), "U2": (256, 64), "D2": (320, 64), "X0": (384, 64), "X1": (448, 64)}
PAIR_FIRST = ("U0", "U1", "D0", "D1")
COPIES = 121
A_ORDER, B_ORDER = (0, 1, 6, 1, 2, 4, 8, 4), (0, 1, 3, 1, 3, 5, 7, 5)


def kernel(a_hbm, b_hbm, c_ref, a_buf, b_buf, relay, load_sem, recv_sem, send_sem):
    row, col = lax.axis_index("row"), lax.axis_index("col")
    y, x_hi = row // 2, row % 2
    x_lo, z, core = col // 8, (col // 2) % 4, col % 2
    x = x_hi * 2 + x_lo

    def device(x, y, z, core):
        return (y * 2 + x // 2, ((x % 2) * 4 + z) * 2 + core)

    z_up, z_down = device(x, y, (z + 1) % 4, core), device(x, y, (z + 3) % 4, core)
    y_up, y_down = device(x, (y + 1) % 4, z, core), device(x, (y + 3) % 4, z, core)
    x_pair = device(x_hi * 2 + 1 - x_lo, y, z, core)
    x_next = device(3 - x, y, z, core)
    twin = device(x, y, z, 1 - core)

    load_a = pltpu.make_async_copy(a_hbm, a_buf.at[0, 0], load_sem.at[0])
    load_b = pltpu.make_async_copy(b_hbm, b_buf.at[0], load_sem.at[1])
    load_a.start()
    load_b.start()

    barrier = pltpu.get_barrier_semaphore()
    for other in (z_up, z_down, y_up, y_down, x_pair, x_next, twin):
        pl.semaphore_signal(barrier, inc=1, device_id=other, device_id_type=MESH)
    c_ref[...] = jnp.zeros_like(c_ref)
    keys, partners = [], []
    for slot in range(8):
        where = ((x_lo + slot // 4) % 2) * 4 + (z + slot % 4) % 4
        d_h, d_y = (where % 2 + x_hi) % 2, (where // 2 + 4 - y) % 4
        partners.append(d_h * 4 + d_y)
        b_order = sum(jnp.where(partners[-1] == other, B_ORDER[other], 0) for other in range(8))
        keys.append(jnp.maximum(b_order, A_ORDER[slot]) * 8 + slot)
    places = [
        sum((keys[other] < keys[slot]).astype(jnp.int32) for other in range(8) if other != slot)
        for slot in range(8)
    ]

    def at_place(place, values):
        return sum(jnp.where(places[slot] == place, values[slot], 0) for slot in range(8))

    chosen = [(at_place(place, range(8)), at_place(place, partners)) for place in range(8)]

    load_a.wait()
    load_b.wait()
    pl.semaphore_wait(barrier, 7)

    sent, arrivals = [], {}

    def arrival(key):
        return recv_sem.at[arrivals.setdefault(key, len(arrivals))]

    def send(src, dst, key, to):
        copy = pltpu.make_async_remote_copy(
            src_ref=src,
            dst_ref=dst,
            send_sem=send_sem.at[len(sent)],
            recv_sem=arrival(key),
            device_id=to,
            device_id_type=MESH,
        )
        copy.start()
        sent.append(copy)

    def wait(ref, key):
        pltpu.make_async_copy(ref, ref, arrival(key)).wait()

    def part(table, first, last):
        return pl.ds(table[first][0], table[last][0] + table[last][1] - table[first][0])

    def a_part(slot, q):
        return a_buf.at[0, slot, part(A_PARTS, q, q)]

    def b_part(slot, q):
        return b_buf.at[slot, part(B_PARTS, q, q)]

    def relay_part(slot, q):
        return relay.at[slot // 2, part(B_PARTS, q, q)]

    def a_send(src, q, slot, to):
        send(a_part(src, q), a_part(slot, q), ("a", slot, q), to)

    def a_wait(slot, q):
        wait(a_part(slot, q), ("a", slot, q))

    def b_send(src, q, slot, to):
        send(b_part(src, q), b_part(slot, q), ("b", slot, q), to)

    def b_wait(slot, q):
        wait(b_part(slot, q), ("b", slot, q))

    def leg_one(slot, q):
        send(b_part(slot, q), relay_part(slot, q), ("r", slot, q), x_pair if pair_first(slot, q) else x_next)

    def relay_wait(slot, q):
        wait(relay_part(slot, q), ("r", slot, q))

    def leg_two(slot, q):
        send(relay_part(slot, q), b_part(4 + slot, q), ("b", 4 + slot, q), x_next if pair_first(slot, q) else x_pair)

    def pair_first(slot, q):
        return q in PAIR_FIRST if slot == 0 else q == "X0"

    def twin_send(slot, first, last):
        at = part(A_PARTS, first, last)
        send(a_buf.at[0, slot, at], a_buf.at[1, slot, at], ("t", slot, first), twin)

    def twin_wait(slot, first, last):
        wait(a_buf.at[1, slot, part(A_PARTS, first, last)], ("t", slot, first))

    def product(place):
        slot, other = chosen[place]
        total = None
        for stream in range(2):
            side = core if stream == 0 else 1 - core
            b = b_buf[other, pl.ds(pl.multiple_of(side * 256, 256), 256)]
            b_top = b.astype(jnp.bfloat16)
            b_low = (b - b_top.astype(jnp.float32)).astype(jnp.bfloat16)
            a = a_buf[stream, slot]
            a_top = a.astype(jnp.bfloat16)
            a_low = (a - a_top.astype(jnp.float32)).astype(jnp.bfloat16)
            dot = functools.partial(jnp.dot, preferred_element_type=jnp.float32)
            part = dot(a_top, b_top) + (dot(a_top, b_low) + dot(a_low, b_top))
            total = part if total is None else total + part
        c_ref[...] += total

    a_send(0, "X0", 3, z_up)
    a_send(0, "U0", 3, z_up)
    a_send(0, "U1", 3, z_up)
    a_send(0, "D0", 3, z_up)
    a_send(0, "D1", 3, z_up)
    a_send(0, "X1", 3, z_up)
    a_send(0, "X1", 1, z_down)
    a_send(0, "D0", 1, z_down)
    a_send(0, "D1", 1, z_down)
    a_send(0, "U0", 1, z_down)
    a_send(0, "U1", 1, z_down)
    a_send(0, "X0", 1, z_down)
    b_send(0, "X0", 3, y_up)
    b_send(0, "U0", 3, y_up)
    b_send(0, "U1", 3, y_up)
    b_send(0, "U2", 3, y_up)
    b_send(0, "D0", 3, y_up)
    b_send(0, "D1", 3, y_up)
    b_send(0, "D2", 3, y_up)
    b_send(0, "X1", 3, y_up)
    b_send(0, "X1", 1, y_down)
    b_send(0, "D0", 1, y_down)
    b_send(0, "D1", 1, y_down)
    b_send(0, "D2", 1, y_down)
    b_send(0, "U0", 1, y_down)
    b_send(0, "U1", 1, y_down)
    b_send(0, "U2", 1, y_down)
    b_send(0, "X0", 1, y_down)
    leg_one(0, "U2")
    leg_one(0, "D2")
    leg_one(0, "X0")
    leg_one(0, "X1")
    leg_one(0, "U0")
    leg_one(0, "D0")
    leg_one(0, "U1")
    leg_one(0, "D1")
    a_send(0, "U0", 4, x_pair)
    a_send(0, "D0", 4, x_pair)
    a_send(0, "U1", 4, x_pair)
    a_send(0, "D1", 4, x_pair)
    twin_send(0, "U0", "X1")
    b_wait(3, "X0")
    b_send(3, "X0", 2, y_up)
    b_wait(1, "X1")
    b_send(1, "X1", 2, y_down)
    relay_wait(0, "U2")
    leg_two(0, "U2")
    a_send(0, "X0", 4, x_pair)
    a_send(0, "X1", 4, x_pair)
    relay_wait(0, "U0")
    leg_two(0, "U0")
    a_wait(3, "X0")
    a_send(3, "X0", 2, z_up)
    a_wait(1, "X1")
    a_send(1, "X1", 2, z_down)
    relay_wait(0, "D2")
    leg_two(0, "D2")
    relay_wait(0, "D0")
    leg_two(0, "D0")
    relay_wait(0, "X0")
    leg_two(0, "X0")
    relay_wait(0, "U1")
    leg_two(0, "U1")
    relay_wait(0, "X1")
    leg_two(0, "X1")
    relay_wait(0, "D1")
    leg_two(0, "D1")
    b_wait(4, "U0")
    b_send(4, "U0", 7, y_up)
    a_wait(4, "U0")
    a_send(4, "U0", 7, z_up)
    b_wait(4, "D0")
    b_send(4, "D0", 7, y_up)
    b_send(4, "D0", 5, y_down)
    b_send(4, "U0", 5, y_down)
    a_wait(4, "D0")
    a_send(4, "D0", 7, z_up)
    a_send(4, "D0", 5, z_down)
    a_send(4, "U0", 5, z_down)
    b_wait(4, "U1")
    b_send(4, "U1", 7, y_up)
    a_wait(4, "U1")
    a_send(4, "U1", 7, z_up)
    a_wait(1, "D0")
    a_wait(1, "D1")
    a_wait(1, "U0")
    a_wait(1, "U1")
    a_wait(1, "X0")
    twin_send(1, "U0", "X1")
    a_wait(3, "U0")
    a_wait(3, "U1")
    a_wait(3, "D0")
    a_wait(3, "D1")
    a_wait(3, "X1")
    twin_send(3, "U0", "X1")
    b_wait(4, "D1")
    b_send(4, "D1", 7, y_up)
    b_wait(3, "U0")
    b_send(3, "U0", 2, y_up)
    b_wait(3, "U1")
    b_send(3, "U1", 2, y_up)
    b_wait(3, "U2")
    b_send(3, "U2", 2, y_up)
    b_send(4, "D1", 5, y_down)
    b_send(4, "U1", 5, y_down)
    b_wait(1, "D0")
    b_send(1, "D0", 2, y_down)
    b_wait(1, "D1")
    b_send(1, "D1", 2, y_down)
    b_wait(1, "D2")
    b_send(1, "D2", 2, y_down)
    a_wait(4, "D1")
    a_send(4, "D1", 7, z_up)
    a_send(4, "D1", 5, z_down)
    a_send(4, "U1", 5, z_down)
    b_wait(2, "X0")
    leg_one(2, "X0")
    b_wait(2, "X1")
    leg_one(2, "X1")
    b_wait(4, "U2")
    b_send(4, "U2", 7, y_up)
    b_send(4, "U2", 5, y_down)
    a_wait(4, "X0")
    a_send(4, "X0", 7, z_up)
    a_send(4, "X0", 5, z_down)
    relay_wait(2, "X1")
    leg_two(2, "X1")
    a_wait(2, "X0")
    a_send(2, "X0", 6, x_pair)
    a_wait(2, "X1")
    a_send(2, "X1", 6, x_pair)
    a_wait(4, "X1")
    a_send(4, "X1", 7, z_up)
    a_send(3, "U0", 2, z_up)
    a_send(3, "U1", 2, z_up)
    a_wait(7, "U0")
    a_send(7, "U0", 6, z_up)
    a_wait(7, "U1")
    a_send(7, "U1", 6, z_up)
    a_send(4, "X1", 5, z_down)
    a_send(1, "D0", 2, z_down)
    a_send(1, "D1", 2, z_down)
    a_wait(5, "D0")
    a_send(5, "D0", 6, z_down)
    a_wait(5, "D1")
    a_send(5, "D1", 6, z_down)
    twin_send(4, "U0", "X1")
    a_wait(7, "D0")
    a_wait(7, "D1")
    twin_send(7, "U0", "D1")
    a_wait(5, "U0")
    a_wait(5, "U1")
    twin_send(5, "U0", "D1")
    b_wait(4, "D2")
    b_send(4, "D2", 7, y_up)
    b_send(4, "D2", 5, y_down)
    twin_wait(0, "U0", "X1")
    b_wait(3, "D0")
    b_wait(1, "U0")
    b_wait(3, "D1")
    b_wait(1, "U1")
    b_wait(3, "D2")
    b_wait(1, "U2")
    b_wait(3, "X1")
    b_wait(1, "X0")
    twin_wait(1, "U0", "X1")
    twin_wait(3, "U0", "X1")
    twin_wait(4, "U0", "X1")
    product(0)
    b_wait(4, "X0")
    b_send(4, "X0", 7, y_up)
    b_send(4, "X0", 5, y_down)
    b_wait(4, "X1")
    b_send(4, "X1", 7, y_up)
    b_wait(7, "U0")
    b_send(7, "U0", 6, y_up)
    b_wait(7, "U1")
    b_send(7, "U1", 6, y_up)
    b_send(4, "X1", 5, y_down)
    b_wait(5, "D0")
    b_send(5, "D0", 6, y_down)
    b_wait(5, "D1")
    b_send(5, "D1", 6, y_down)
    b_wait(2, "U0")
    b_wait(2, "D0")
    b_wait(2, "U1")
    b_wait(2, "D1")
    b_wait(2, "U2")
    b_wait(2, "D2")
    product(1)
    b_wait(7, "U2")
    b_send(7, "U2", 6, y_up)
    relay_wait(2, "X0")
    leg_two(2, "X0")
    a_wait(7, "X0")
    a_wait(7, "X1")
    twin_send(7, "X0", "X1")
    a_wait(5, "X0")
    a_wait(5, "X1")
    twin_send(5, "X0", "X1")
    b_wait(5, "D2")
    b_send(5, "D2", 6, y_down)
    twin_wait(7, "U0", "D1")
    twin_wait(5, "U0", "D1")
    twin_wait(7, "X0", "X1")
    twin_wait(5, "X0", "X1")
    product(2)
    a_wait(2, "U0")
    a_wait(2, "D0")
    a_wait(2, "U1")
    a_wait(2, "D1")
    twin_send(2, "U0", "X1")
    a_wait(6, "X0")
    twin_send(6, "X0", "X0")
    b_wait(7, "D0")
    b_wait(5, "U0")
    b_wait(7, "D1")
    b_wait(5, "U1")
    b_wait(5, "U2")
    b_wait(7, "D2")
    b_wait(7, "X0")
    b_wait(5, "X0")
    b_wait(7, "X1")
    b_wait(5, "X1")
    product(3)
    product(4)
    twin_wait(2, "U0", "X1")
    product(5)
    a_wait(6, "U0")
    a_wait(6, "U1")
    twin_send(6, "U0", "U1")
    a_wait(6, "D0")
    a_wait(6, "D1")
    twin_send(6, "D0", "D1")
    a_wait(6, "X1")
    twin_send(6, "X1", "X1")
    b_wait(6, "X1")
    b_wait(6, "X0")
    b_wait(6, "U0")
    b_wait(6, "D0")
    b_wait(6, "U1")
    b_wait(6, "D1")
    b_wait(6, "U2")
    b_wait(6, "D2")
    product(6)
    twin_wait(6, "X0", "X0")
    twin_wait(6, "U0", "U1")
    twin_wait(6, "D0", "D1")
    twin_wait(6, "X1", "X1")
    product(7)
    for copy in sent:
        copy.wait_send()


def body(left_matrix, right_matrix):
    kept = functools.partial(pltpu.with_memory_space_constraint, memory_space=pltpu.HBM)
    return pl.pallas_call(
        kernel,
        out_shape=jax.ShapeDtypeStruct((ROWS, COLUMNS), jnp.float32),
        in_specs=[pl.BlockSpec(memory_space=pl.ANY)] * 2,
        out_specs=pl.BlockSpec(memory_space=pltpu.VMEM),
        scratch_shapes=[
            pltpu.VMEM((2, 8, ROWS, COLUMNS), jnp.float32),
            pltpu.VMEM((8, ROWS, COLUMNS), jnp.float32),
            pltpu.VMEM((2, ROWS, COLUMNS), jnp.float32),
            pltpu.SemaphoreType.DMA((2,)),
            pltpu.SemaphoreType.DMA((COPIES,)),
            pltpu.SemaphoreType.DMA((COPIES,)),
        ],
        compiler_params=pltpu.CompilerParams(
            collective_id=0, has_side_effects=True, vmem_limit_bytes=24 * 2**20
        ),
    )(kept(left_matrix), kept(right_matrix))


def solution(mesh):
    placed = (P("row", "col"), P("row", "col"))
    return jax.shard_map(
        body, mesh=mesh, in_specs=placed, out_specs=P("row", "col"), check_vma=False
    )
```

time: 123 us -> 46.3 us (0.38)
  blocking collectives: 96.2 us -> 0 us
  Pallas kernels: 0 us -> 45.4 us
  between operations: 13.4 us -> 0.01 us
  matrix products: 10.6 us -> 0 us
    all_to_all x1 -> x0, blocking collectives: 96.2 us -> none  [copy_for_each(): lax.all_to_all(jnp.broadcast_to(array[None], (devices, *array.shape)), ax...]
    pallas_call x0 -> x1, Pallas kernels: none -> 45.4 us  [body(): pl.pallas_call(kernel, out_shape=jax.ShapeDtypeStruct((ROWS, COLUMNS), jn...]
    dot_general x1 -> x0, matrix products: 10.6 us -> none  [multiply(): jnp.dot(left_term, right_term, precision=lax.Precision.HIGHEST, preferred...]
    broadcast_in_dim x1 -> x0, local copies, waits for them, and re-layouts: 1.4 us -> none  [copy_for_each(): jnp.broadcast_to(array[None], (devices, *array.shape))]
  transfers between devices with their start and end apart: 1 -> 0, of which waited for: 0 -> 0; matrix products, arithmetic and copies ran while one was open for 1% -> 0% of each run, Pallas kernels for 0% -> 0%
where the time goes in v2:
time: 46.3 us; the launch traced here: 46.2 us
  Pallas kernels  45.4 us (98%)
  local copies, waits for them, and re-layouts  0.8 us (2%)
    pallas_call x1, Pallas kernels, body(): pl.pallas_call(kernel, out_shape=jax.ShapeDtypeStruct((ROWS, COLUMNS), jn...  45.4 us

profile of v2, /device:TPU:1, one launch (start us, length us, event | category | flops | bytes accessed | tf_op | source)
XLA Modules:
  0.0 46.2 jit_solution(14794993347056585473)
XLA Ops:
  0.0 45.4 %shard_map.28 = f32[512,256]{1,0:T(8,128)S(1)} custom-call(f32[512,256]{1,0:T(8,128)} %a_hbm.1, f32[512,256]{1,0:T(8,128)} %b_hbm.1), custom_call_target="tpu_custom_call" | custom-call | tf_op jit(solution)/shard_map/pallas_call | solution.py:399
  45.4 0.8 %copy.4 = f32[512,256]{1,0:T(8,128)} copy(f32[512,256]{1,0:T(8,128)S(1)} %shard_map.28) | data formatting | bytes 1048576
